TPU v7x, 32 devices: a whole 2x2x4 slice. The times are simulated.
32 devices in a mesh: section: 4 (over z), node: 4 (over x, core), local: 2 (over y).
Axes of the slice: x: 2, y: 2, z: 4, core: 2. Of those that a mesh axis runs over, the one named last changes fastest.
Arguments:
- tokens: bfloat16 [4, 768, 7168], P('section', ('node', 'local')), may hold values from -6 to 6
- routes: int32 [4, 768, 8], P('section', ('node', 'local')), may hold values from 0 to 383, as said below
- route_gates: float32 [4, 768, 8], P('section', ('node', 'local')), may hold values from 0.2 to 1
- replica_table: int32 [4], replicated, may hold values from 0 to 2, as said below
- w_gate: bfloat16 [4, 7168, 256], P('node', None, 'local')
- w_up: bfloat16 [4, 7168, 256], P('node', None, 'local')
- w_down: bfloat16 [4, 256, 7168], P('node', 'local')
Outputs:
- section_input: bfloat16 [4, 768, 7168], P('section', ('node', 'local'))
Inputs may be any that keep to these rules, and one draw needn't show every extreme that they name: `replica_table`: each of the experts 0 to 2 is held by one or two slots; slots that hold the same expert hold equal weights in w_gate, w_up and w_down. `routes`: each row names 8 different experts. Within the rows of one device, expert e < 3 is named by at least one row and by at most 2 times its number of slots in replica_table; in every draw some expert with one slot is named by exactly 2 rows of every device.
All inputs are finite; a program needn't handle non-finite values.
Results may differ from a plain program's by a relative error of at most 0.015.
Values may be sent and summed in bfloat16 or wider, within the bound.
A program may use at most 64 MiB of HBM per device.

v0:
```python
import functools

import jax
import jax.numpy as jnp
from jax import lax
from jax.experimental import pallas as pl
from jax.experimental.pallas import tpu as pltpu
from jax.sharding import PartitionSpec as P

CAP = 2
G = 8
B = CAP * G
KEEP = 61000 * 1024
SPLIT = 4
MESH = pl.DeviceIdType.MESH


def row_piece(shape):
    return lax.broadcasted_iota(jnp.int32, shape, 0) % G


def relay_kernel(
    n_section, n_node, n_local,
    table_hbm, routes_hbm, gates_hbm, tok_hbm, wg_hbm, wu_hbm, wd_hbm,
    rows_ref, mix_ref,
    table_ref, routes_ref, gates_ref, ids, vals, tok, wg, wu, wd, disp, recv, outb, ret, comb_own, comb_in,
    in_sem, tok_sem, w_sem, send_sem, recv_sem, back_sem, ret_sem, comb_send, comb_recv,
):
    s = lax.axis_index("section")
    n = lax.axis_index("node")
    l = lax.axis_index("local")
    odd = n % 2
    sources = n_node * n_local
    me = n * n_local + l
    tok_dev, width = tok_hbm.shape
    piece = width // G
    tok_pad = ids.shape[1]
    hid = wg_hbm.shape[1]
    sends = s < n_section - 1
    owns = s > 0
    works = jnp.logical_and(s + odd > 0, s + odd < n_section)

    others = sorted(
        ((dn, dl) for dn in range(n_node) for dl in range(n_local) if dn or dl),
        key=lambda d: (d[0] == 0) + (d[1] == 0) + (d[0] % 2) / 4,
    )

    def cols(k):
        return pl.ds(k * piece, piece)

    tok_copies = [
        pltpu.make_async_copy(
            tok_hbm.at[:, cols(k)], tok.at[pl.ds(k * tok_pad, tok_dev)], tok_sem.at[k]
        )
        for k in range(G)
    ]
    w_copies = [
        pltpu.make_async_copy(
            hbm.at[pl.ds(i * hbm.shape[0] // SPLIT, hbm.shape[0] // SPLIT)],
            held.at[pl.ds(i * hbm.shape[0] // SPLIT, hbm.shape[0] // SPLIT)],
            w_sem.at[w * SPLIT + i],
        )
        for w, (hbm, held) in enumerate(((wg_hbm, wg), (wu_hbm, wu), (wd_hbm, wd)))
        for i in range(SPLIT)
    ]
    in_copies = [
        pltpu.make_async_copy(table_hbm, table_ref, in_sem.at[0]),
        pltpu.make_async_copy(routes_hbm, routes_ref, in_sem.at[1]),
        pltpu.make_async_copy(gates_hbm, gates_ref, in_sem.at[2]),
    ]

    barrier = pltpu.get_barrier_semaphore()

    def greet(section, places):
        for dn, dl in places:
            pl.semaphore_signal(
                barrier, inc=1,
                device_id=(section, (n + dn) % n_node, (l + dl) % n_local),
                device_id_type=MESH,
            )

    @pl.when(owns)
    def _():
        greet(s - 1, others + [(0, 0)])

    greet(s, others)
    for c in in_copies + tok_copies:
        c.start()
    for c in in_copies:
        c.wait()

    ids[...] = jnp.full(ids.shape, -1, jnp.int32)
    vals[...] = jnp.zeros(vals.shape, jnp.float32)
    ids[:, :tok_dev] = routes_ref[...]
    vals[:, :tok_dev] = gates_ref[...]
    picks = ids[...]
    gates = vals[...]
    named_rows = max(16, n_node)
    row_id = lax.broadcasted_iota(jnp.int32, (named_rows, tok_pad), 0)
    named = jnp.zeros((named_rows, tok_pad), jnp.float32)
    hits, weights = [], []
    for j in range(n_node):
        hit = picks == table_ref[j]
        hits.append(jnp.max(jnp.where(hit, 1.0, 0.0), axis=0, keepdims=True))
        weights.append(jnp.sum(jnp.where(hit, gates, 0.0), axis=0, keepdims=True))
        named = jnp.where(row_id == j, hits[j], named)
    before = lax.broadcasted_iota(jnp.int32, (tok_pad, tok_pad), 0) < lax.broadcasted_iota(
        jnp.int32, (tok_pad, tok_pad), 1
    )
    rank = jnp.dot(
        named.astype(jnp.bfloat16),
        jnp.where(before, 1.0, 0.0).astype(jnp.bfloat16),
        preferred_element_type=jnp.float32,
    ).astype(jnp.int32)
    chosen = []
    for j in range(n_node):
        copies = jnp.int32(0)
        replica = jnp.int32(0)
        for i in range(n_node):
            same = (table_ref[i] == table_ref[j]).astype(jnp.int32)
            copies = copies + same
            if i < j:
                replica = replica + same
        for p in range(CAP):
            want = p * copies + replica
            sel = jnp.where(rank[j : j + 1] == want, hits[j], 0.0)
            comb_own[j * CAP + p : j * CAP + p + 1, :] = sel * weights[j]
            chosen.append(jnp.broadcast_to(sel, (G, tok_pad)))
    chosen = jnp.concatenate(chosen, axis=0)
    piece_of = row_piece(chosen.shape)
    select = jnp.concatenate(
        [jnp.where(piece_of == k, chosen, 0.0).astype(jnp.bfloat16) for k in range(G)], axis=1
    )
    if tok_pad > tok_dev:
        for k in range(G):
            tok[k * tok_pad + tok_dev : (k + 1) * tok_pad, :] = jnp.zeros(
                (tok_pad - tok_dev, piece), jnp.bfloat16
            )
    for c in tok_copies:
        c.wait()
    for c in w_copies:
        c.start()
    disp[...] = jnp.dot(select, tok[...], preferred_element_type=jnp.float32).astype(jnp.bfloat16)

    around = (sources - 1) + sources * sends.astype(jnp.int32)
    pl.semaphore_wait(barrier, around)

    def dispatch(dn, dl):
        j = (n + dn) % n_node
        m = (l + dl) % n_local
        return pltpu.make_async_remote_copy(
            src_ref=disp.at[pl.ds(pl.multiple_of(j * B, B), B)],
            dst_ref=recv.at[pl.ds(pl.multiple_of(me * B, B), B)],
            send_sem=send_sem.at[dn * n_local + dl],
            recv_sem=recv_sem.at[me],
            device_id=(s + 1 - j % 2, j, m),
            device_id_type=MESH,
        )

    own_in = pltpu.make_async_copy(
        disp.at[pl.ds(pl.multiple_of(n * B, B), B)],
        recv.at[pl.ds(pl.multiple_of(me * B, B), B)],
        recv_sem.at[me],
    )
    comb_copy = pltpu.make_async_remote_copy(
        src_ref=comb_own, dst_ref=comb_in, send_sem=comb_send.at[0], recv_sem=comb_recv.at[0],
        device_id=(s + 1, n, l), device_id_type=MESH,
    )
    @pl.when(sends)
    def _():
        for dn, dl in others:
            dispatch(dn, dl).start()

        @pl.when(odd == 0)
        def _():
            dispatch(0, 0).start()

        @pl.when(odd == 1)
        def _():
            own_in.start()

        comb_copy.start()

    def give_back(dn, dl):
        qn = (n + dn) % n_node
        ql = (l + dl) % n_local
        q = qn * n_local + ql
        return pltpu.make_async_remote_copy(
            src_ref=outb.at[pl.ds(pl.multiple_of(q * B, B), B)],
            dst_ref=ret.at[l, pl.ds(pl.multiple_of(n * B, B), B)],
            send_sem=back_sem.at[dn * n_local + dl],
            recv_sem=ret_sem.at[me],
            device_id=(s + odd, qn, ql),
            device_id_type=MESH,
        )

    own_back = pltpu.make_async_copy(
        outb.at[pl.ds(pl.multiple_of(me * B, B), B)],
        ret.at[l, pl.ds(pl.multiple_of(n * B, B), B)],
        ret_sem.at[me],
    )

    for c in w_copies:
        c.wait()

    @pl.when(works)
    def _():
        for q in range(sources):
            block = recv.at[pl.ds(q * B, B)]
            pltpu.make_async_copy(block, block, recv_sem.at[q]).wait()
        rows = recv[...]
        piece_id = row_piece((sources * B, 2 * hid))
        total = jnp.zeros((sources * B, 2 * hid), jnp.float32)
        for k in range(G):
            both = jnp.concatenate(
                [wg[k * piece : (k + 1) * piece, :], wu[k * piece : (k + 1) * piece, :]], axis=1
            )
            part = jnp.dot(rows, both, preferred_element_type=jnp.float32)
            total = total + jnp.where(piece_id == k, part, 0.0)
        total = total.reshape(sources * CAP, G, 2 * hid)
        total = jnp.broadcast_to(jnp.sum(total, axis=1, keepdims=True), total.shape)
        total = total.reshape(sources * B, 2 * hid)
        gate_proj = total[:, :hid]
        up_proj = total[:, hid:]
        hidden = gate_proj / (1.0 + jnp.exp(-gate_proj)) * up_proj
        piece_h = row_piece(hidden.shape)
        spread = jnp.concatenate(
            [jnp.where(piece_h == k, hidden, 0.0).astype(jnp.bfloat16) for k in range(G)], axis=1
        )
        down = jnp.concatenate([wd[:, k * piece : (k + 1) * piece] for k in range(G)], axis=0)
        outb[...] = jnp.dot(spread, down, preferred_element_type=jnp.float32).astype(
            jnp.bfloat16
        )
        for dn, dl in others:
            give_back(dn, dl).start()

        @pl.when(odd == 1)
        def _():
            give_back(0, 0).start()

        @pl.when(odd == 0)
        def _():
            own_back.start()

    @pl.when(owns)
    def _():
        comb_copy.wait_recv()
        mix = comb_in[...]
        high = mix.astype(jnp.bfloat16).astype(jnp.float32)
        tall = jnp.concatenate(
            [
                jnp.broadcast_to(part[c : c + 1], (G, tok_pad))
                for part in (high, mix - high)
                for c in range(n_node * CAP)
            ],
            axis=0,
        )
        mix_ref[...] = jnp.transpose(tall).astype(jnp.bfloat16)
        for q in range(sources):
            block = ret.at[q % n_local, pl.ds((q // n_local) * B, B)]
            pltpu.make_async_copy(block, block, ret_sem.at[q]).wait()
        summed = ret[0].astype(jnp.float32)
        for m in range(1, n_local):
            summed = summed + ret[m].astype(jnp.float32)
        rows_ref[...] = summed.astype(jnp.bfloat16)

    @pl.when(s == 0)
    def _():
        rows_ref[...] = jnp.zeros(rows_ref.shape, jnp.bfloat16)
        mix_ref[...] = jnp.zeros(mix_ref.shape, jnp.bfloat16)

    @pl.when(sends)
    def _():
        for dn, dl in others:
            dispatch(dn, dl).wait_send()

        @pl.when(odd == 0)
        def _():
            dispatch(0, 0).wait_send()

        comb_copy.wait_send()

    @pl.when(works)
    def _():
        for dn, dl in others:
            give_back(dn, dl).wait_send()

        @pl.when(odd == 1)
        def _():
            give_back(0, 0).wait_send()


def expand_kernel(rows_ref, mix_ref, out_hbm, obuf, sem):
    tok_dev = out_hbm.shape[0]
    piece = rows_ref.shape[1]
    rows = rows_ref[...]
    rows = jnp.concatenate([rows, rows], axis=0)
    mix = mix_ref[:tok_dev, :].astype(jnp.float32)
    lane = lax.broadcasted_iota(jnp.int32, mix.shape, 1) % G
    copies = []
    for k in range(G):
        left = jnp.where(lane == k, mix, 0.0).astype(jnp.bfloat16)
        obuf[k] = jnp.dot(left, rows, preferred_element_type=jnp.float32).astype(jnp.bfloat16)
        copy = pltpu.make_async_copy(
            obuf.at[k], out_hbm.at[:, pl.ds(k * piece, piece)], sem.at[k]
        )
        copy.start()
        copies.append(copy)
    for copy in copies:
        copy.wait()


def shards(n_section, tokens, routes, route_gates, replica_table, w_gate, w_up, w_down):
    n_node = lax.axis_size("node")
    n_local = lax.axis_size("local")
    sources = n_node * n_local
    tok_dev, width = tokens.shape[1:]
    topk = routes.shape[2]
    hid = w_gate.shape[2]
    piece = width // G
    tok_pad = -(-tok_dev // 128) * 128
    slots = n_node * CAP
    vmem = pl.BlockSpec(memory_space=pltpu.VMEM)
    hbm = pl.BlockSpec(memory_space=pltpu.HBM)
    rows, mix = pl.pallas_call(
        functools.partial(relay_kernel, n_section, n_node, n_local),
        out_shape=(
            jax.ShapeDtypeStruct((n_node * B, piece), jnp.bfloat16),
            jax.ShapeDtypeStruct((tok_pad, 2 * slots * G), jnp.bfloat16),
        ),
        in_specs=[hbm] * 7,
        out_specs=(vmem, vmem),
        scratch_shapes=[
            pltpu.SMEM((n_node,), jnp.int32),
            pltpu.VMEM((topk, tok_dev), jnp.int32),
            pltpu.VMEM((topk, tok_dev), jnp.float32),
            pltpu.VMEM((topk, tok_pad), jnp.int32),
            pltpu.VMEM((topk, tok_pad), jnp.float32),
            pltpu.VMEM((G * tok_pad, piece), jnp.bfloat16),
            pltpu.VMEM((width, hid), jnp.bfloat16),
            pltpu.VMEM((width, hid), jnp.bfloat16),
            pltpu.VMEM((hid, width), jnp.bfloat16),
            pltpu.VMEM((n_node * B, piece), jnp.bfloat16),
            pltpu.VMEM((sources * B, piece), jnp.bfloat16),
            pltpu.VMEM((sources * B, piece), jnp.bfloat16),
            pltpu.VMEM((n_local, n_node * B, piece), jnp.bfloat16),
            pltpu.VMEM((slots, tok_pad), jnp.float32),
            pltpu.VMEM((slots, tok_pad), jnp.float32),
            pltpu.SemaphoreType.DMA((3,)),
            pltpu.SemaphoreType.DMA((G,)),
            pltpu.SemaphoreType.DMA((3 * SPLIT,)),
            pltpu.SemaphoreType.DMA((sources,)),
            pltpu.SemaphoreType.DMA((sources,)),
            pltpu.SemaphoreType.DMA((sources,)),
            pltpu.SemaphoreType.DMA((sources,)),
            pltpu.SemaphoreType.DMA((1,)),
            pltpu.SemaphoreType.DMA((1,)),
        ],
        compiler_params=pltpu.CompilerParams(
            collective_id=0, has_side_effects=True, vmem_limit_bytes=KEEP
        ),
        name="relay",
    )(
        replica_table,
        jnp.transpose(routes[0]),
        jnp.transpose(route_gates[0]),
        tokens[0],
        w_gate[0],
        w_up[0],
        w_down[0],
    )
    out = pl.pallas_call(
        expand_kernel,
        out_shape=jax.ShapeDtypeStruct((tok_dev, width), jnp.bfloat16),
        in_specs=[vmem, vmem],
        out_specs=hbm,
        scratch_shapes=[
            pltpu.VMEM((G, tok_dev, piece), jnp.bfloat16),
            pltpu.SemaphoreType.DMA((G,)),
        ],
        compiler_params=pltpu.CompilerParams(vmem_limit_bytes=KEEP),
        name="expand",
    )(rows, mix)
    return out[None]


def solution(mesh):
    placed = (
        P("section", ("node", "local"), None),
        P("section", ("node", "local"), None),
        P("section", ("node", "local"), None),
        P(),
        P("node", None, "local"),
        P("node", None, "local"),
        P("node", "local", None),
    )
    return jax.shard_map(
        functools.partial(shards, mesh.shape["section"]),
        mesh=mesh,
        in_specs=placed,
        out_specs=P("section", ("node", "local"), None),
        check_vma=False,
    )
```

profile of v0, /device:TPU:17, one launch (start us, length us, event | category | flops | bytes accessed | tf_op | source)
XLA Modules:
  0.0 16.9 jit_solution(16950826194295451785)
XLA Ops:
  0.0 14.7 %relay.1 = (bf16[64,896]{1,0:T(8,128)(2,1)}, bf16[128,128]{1,0:T(8,128)(2,1)}) custom-call(s32[4]{0:T(128)} %table_hbm.1, s32[8,96]{1,0:T(8,128)} %bitcast.15, f32[8,96]{1,0:T(8,128)} %bitcast.16, bf16[96,7168]{1,0:T(8,128)(2,1)} %bitcast.14, bf16[7168,128]{1,0:T(8,128)(2,1)} %bitcast.11, bf16[7168,128]{1,0:T(8,128)(2,1)} %bitcast.12, bf16[128,7168]{1,0:T(8,128)(2,1)} %bitcast.13), custom_call_target="tpu_custom_call" | custom-call | tf_op jit(solution)/shard_map/relay/pallas_call | solution.py:325
  14.7 2.2 %expand.1 = bf16[96,7168]{1,0:T(8,128)(2,1)} custom-call(bf16[64,896]{1,0:T(8,128)(2,1)} %get-tuple-element.7.rows_ref, bf16[128,128]{1,0:T(8,128)(2,1)} %get-tuple-element.8.mix_ref), custom_call_target="tpu_custom_call" | custom-call | tf_op jit(solution)/shard_map/expand/pallas_call | solution.py:372
where the time goes:
time: 17.1 us; the launch traced here: 16.9 us
  Pallas kernels  16.9 us (99%)
    pallas_call x1, Pallas kernels, shards(): pl.pallas_call(functools.partial(relay_kernel, n_section, n_node, n_local...  14.7 us
    pallas_call x1, Pallas kernels, shards(): pl.pallas_call(expand_kernel, out_shape=jax.ShapeDtypeStruct((tok_dev, wi...  2.24 us

commit v1 on v0

--- a/solution.py
+++ b/solution.py
@@ -10,7 +10,7 @@
 CAP = 2
 G = 8
 B = CAP * G
-KEEP = 61000 * 1024
+KEEP = 24 * 1024 * 1024
 SPLIT = 4
 MESH = pl.DeviceIdType.MESH
 
@@ -325,8 +325,8 @@
     rows, mix = pl.pallas_call(
         functools.partial(relay_kernel, n_section, n_node, n_local),
         out_shape=(
-            jax.ShapeDtypeStruct((n_node * B, piece), jnp.bfloat16),
-            jax.ShapeDtypeStruct((tok_pad, 2 * slots * G), jnp.bfloat16),
+            pltpu.VMEM((n_node * B, piece), jnp.bfloat16),
+            pltpu.VMEM((tok_pad, 2 * slots * G), jnp.bfloat16),
         ),
         in_specs=[hbm] * 7,
         out_specs=(vmem, vmem),
@@ -361,13 +361,18 @@
         ),
         name="relay",
     )(
-        replica_table,
-        jnp.transpose(routes[0]),
-        jnp.transpose(route_gates[0]),
-        tokens[0],
-        w_gate[0],
-        w_up[0],
-        w_down[0],
+        *(
+            pltpu.with_memory_space_constraint(a, pltpu.HBM)
+            for a in (
+                replica_table,
+                jnp.transpose(routes[0]),
+                jnp.transpose(route_gates[0]),
+                tokens[0],
+                w_gate[0],
+                w_up[0],
+                w_down[0],
+            )
+        )
     )
     out = pl.pallas_call(
         expand_kernel,

time: 17.1 us -> 15.5 us (0.906)
  Pallas kernels: 16.9 us -> 15.4 us
    pallas_call x1, Pallas kernels: 2.24 us -> 1.34 us  [shards(): pl.pallas_call(expand_kernel, out_shape=jax.ShapeDtypeStruct((tok_dev, wi...]
    pallas_call x1, Pallas kernels: 14.7 us -> 14 us  [shards(): pl.pallas_call(functools.partial(relay_kernel, n_section, n_node, n_local...]
where the time goes in v1:
time: 15.5 us; the launch traced here: 15.4 us
  Pallas kernels  15.4 us (99%)
    pallas_call x1, Pallas kernels, shards(): pl.pallas_call(functools.partial(relay_kernel, n_section, n_node, n_local...  14 us
    pallas_call x1, Pallas kernels, shards(): pl.pallas_call(expand_kernel, out_shape=jax.ShapeDtypeStruct((tok_dev, wi...  1.34 us

profile of v1, /device:TPU:17, one launch (start us, length us, event | category | flops | bytes accessed | tf_op | source)
XLA Modules:
  0.0 15.4 jit_solution(9635977287909942321)
XLA Ops:
  0.0 14.0 %relay.1 = (bf16[64,896]{1,0:T(8,128)(2,1)S(1)}, bf16[128,128]{1,0:T(8,128)(2,1)S(1)}) custom-call(s32[4]{0:T(128)} %table_hbm.1, s32[8,96]{1,0:T(8,128)} %bitcast.15, f32[8,96]{1,0:T(8,128)} %bitcast.16, bf16[96,7168]{1,0:T(8,128)(2,1)} %bitcast.14, bf16[7168,128]{1,0:T(8,128)(2,1)} %bitcast.11, bf16[7168,128]{1,0:T(8,128)(2,1)} %bitcast.12, ...), custom_call_target="tpu_custom_call" | custom-call | tf_op jit(solution)/shard_map/relay/pallas_call | solution.py:325
  14.0 1.3 %expand.1 = bf16[96,7168]{1,0:T(8,128)(2,1)} custom-call(bf16[64,896]{1,0:T(8,128)(2,1)S(1)} %get-tuple-element.7.rows_ref, bf16[128,128]{1,0:T(8,128)(2,1)S(1)} %get-tuple-element.8.mix_ref), custom_call_target="tpu_custom_call" | custom-call | tf_op jit(solution)/shard_map/expand/pallas_call | solution.py:377

commit v2 on v1

--- a/solution.py
+++ b/solution.py
@@ -24,26 +24,36 @@
     table_hbm, routes_hbm, gates_hbm, tok_hbm, wg_hbm, wu_hbm, wd_hbm,
     rows_ref, mix_ref,
     table_ref, routes_ref, gates_ref, ids, vals, tok, wg, wu, wd, disp, recv, outb, ret, comb_own, comb_in,
-    in_sem, tok_sem, w_sem, send_sem, recv_sem, back_sem, ret_sem, comb_send, comb_recv,
+    in_sem, tok_sem, w_sem, send_sem, recv_sem, back_sem, ret_sem, comb_send, comb_recv, up_sem,
 ):
     s = lax.axis_index("section")
     n = lax.axis_index("node")
     l = lax.axis_index("local")
-    odd = n % 2
+    core = n % 2
+    chips = n_node // 2
     sources = n_node * n_local
-    me = n * n_local + l
     tok_dev, width = tok_hbm.shape
     piece = width // G
     tok_pad = ids.shape[1]
     hid = wg_hbm.shape[1]
     sends = s < n_section - 1
     owns = s > 0
-    works = jnp.logical_and(s + odd > 0, s + odd < n_section)
-
-    others = sorted(
-        ((dn, dl) for dn in range(n_node) for dl in range(n_local) if dn or dl),
-        key=lambda d: (d[0] == 0) + (d[1] == 0) + (d[0] % 2) / 4,
-    )
+
+    home = (0, 0)
+    moves = sorted(
+        ((dx, dl) for dx in range(chips) for dl in range(n_local)),
+        key=lambda d: -min(d[0], chips - d[0]) - min(d[1], n_local - d[1]),
+    )
+    here = [d for d in moves if (d[0] + d[1]) % 2 == 0]
+    above = [d for d in moves if (d[0] + d[1]) % 2 == 1]
+    slots = here + above
+    near_rows = len(here) * 2 * B
+
+    def place(move, side):
+        return (n // 2 + move[0]) % chips * 2 + side, (l + move[1]) % n_local
+
+    def back(move):
+        return -move[0], -move[1]
 
     def cols(k):
         return pl.ds(k * piece, piece)
@@ -71,19 +81,26 @@
 
     barrier = pltpu.get_barrier_semaphore()
 
-    def greet(section, places):
-        for dn, dl in places:
-            pl.semaphore_signal(
-                barrier, inc=1,
-                device_id=(section, (n + dn) % n_node, (l + dl) % n_local),
-                device_id_type=MESH,
-            )
-
-    @pl.when(owns)
-    def _():
-        greet(s - 1, others + [(0, 0)])
-
-    greet(s, others)
+    def greet(section, move, side):
+        j, m = place(move, side)
+        pl.semaphore_signal(barrier, inc=1, device_id=(section, j, m), device_id_type=MESH)
+
+    for move in moves:
+        for flip in range(2):
+            if move != home or flip:
+                greet(s, move, core ^ flip)
+
+    callers = [(back(move), flip) for move in above for flip in range(2)] + [(home, 0)]
+
+    @pl.when(owns)
+    def _():
+        for move, flip in callers:
+            greet(s - 1, move, core ^ flip)
+
+    @pl.when(sends)
+    def _():
+        greet(s + 1, home, core)
+
     for c in in_copies + tok_copies:
         c.start()
     for c in in_copies:
@@ -140,107 +157,115 @@
         c.wait()
     for c in w_copies:
         c.start()
-    disp[...] = jnp.dot(select, tok[...], preferred_element_type=jnp.float32).astype(jnp.bfloat16)
-
-    around = (sources - 1) + sources * sends.astype(jnp.int32)
-    pl.semaphore_wait(barrier, around)
-
-    def dispatch(dn, dl):
-        j = (n + dn) % n_node
-        m = (l + dl) % n_local
+    def dispatch(move, side, up):
+        j, m = place(move, side)
         return pltpu.make_async_remote_copy(
             src_ref=disp.at[pl.ds(pl.multiple_of(j * B, B), B)],
-            dst_ref=recv.at[pl.ds(pl.multiple_of(me * B, B), B)],
-            send_sem=send_sem.at[dn * n_local + dl],
-            recv_sem=recv_sem.at[me],
-            device_id=(s + 1 - j % 2, j, m),
+            dst_ref=recv.at[block_of(move, core)],
+            send_sem=send_sem.at[0],
+            recv_sem=recv_sem.at[up],
+            device_id=(s + up, j, m),
             device_id_type=MESH,
         )
 
-    own_in = pltpu.make_async_copy(
-        disp.at[pl.ds(pl.multiple_of(n * B, B), B)],
-        recv.at[pl.ds(pl.multiple_of(me * B, B), B)],
-        recv_sem.at[me],
-    )
+    def block_of(move, side):
+        return pl.ds(pl.multiple_of((slots.index(move) * 2 + side) * B, B), B)
+
+    def own_in():
+        return pltpu.make_async_copy(
+            disp.at[pl.ds(pl.multiple_of(n * B, B), B)],
+            recv.at[block_of(home, core)],
+            recv_sem.at[0],
+        )
+
     comb_copy = pltpu.make_async_remote_copy(
         src_ref=comb_own, dst_ref=comb_in, send_sem=comb_send.at[0], recv_sem=comb_recv.at[0],
         device_id=(s + 1, n, l), device_id_type=MESH,
     )
+    disp[...] = jnp.dot(select, tok[...], preferred_element_type=jnp.float32).astype(
+        jnp.bfloat16
+    )
+    pl.semaphore_wait(
+        barrier,
+        sources - 1 + len(callers) * sends.astype(jnp.int32) + owns.astype(jnp.int32),
+    )
+
+    @pl.when(owns)
+    def _():
+        pl.semaphore_signal(up_sem, inc=1, device_id=(s - 1, n, l), device_id_type=MESH)
+
     @pl.when(sends)
     def _():
-        for dn, dl in others:
-            dispatch(dn, dl).start()
-
-        @pl.when(odd == 0)
-        def _():
-            dispatch(0, 0).start()
-
-        @pl.when(odd == 1)
-        def _():
-            own_in.start()
-
         comb_copy.start()
-
-    def give_back(dn, dl):
-        qn = (n + dn) % n_node
-        ql = (l + dl) % n_local
-        q = qn * n_local + ql
+        for move in here:
+            for side in range(2):
+                if move != home:
+                    dispatch(move, side, 0).start()
+        for move in above:
+            for side in range(2):
+                dispatch(move, side, 1).start()
+        dispatch(home, 1 - core, 0).start()
+        own_in().start()
+
+    def give_back(move, side, up):
+        qn, ql = place(back(move), side)
         return pltpu.make_async_remote_copy(
-            src_ref=outb.at[pl.ds(pl.multiple_of(q * B, B), B)],
+            src_ref=outb.at[block_of(move, side)],
             dst_ref=ret.at[l, pl.ds(pl.multiple_of(n * B, B), B)],
-            send_sem=back_sem.at[dn * n_local + dl],
-            recv_sem=ret_sem.at[me],
-            device_id=(s + odd, qn, ql),
+            send_sem=back_sem.at[1 - up],
+            recv_sem=ret_sem.at[0],
+            device_id=(s + up, qn, ql),
             device_id_type=MESH,
         )
-
-    own_back = pltpu.make_async_copy(
-        outb.at[pl.ds(pl.multiple_of(me * B, B), B)],
-        ret.at[l, pl.ds(pl.multiple_of(n * B, B), B)],
-        ret_sem.at[me],
-    )
 
     for c in w_copies:
         c.wait()
 
-    @pl.when(works)
-    def _():
-        for q in range(sources):
-            block = recv.at[pl.ds(q * B, B)]
-            pltpu.make_async_copy(block, block, recv_sem.at[q]).wait()
-        rows = recv[...]
-        piece_id = row_piece((sources * B, 2 * hid))
-        total = jnp.zeros((sources * B, 2 * hid), jnp.float32)
-        for k in range(G):
-            both = jnp.concatenate(
-                [wg[k * piece : (k + 1) * piece, :], wu[k * piece : (k + 1) * piece, :]], axis=1
-            )
-            part = jnp.dot(rows, both, preferred_element_type=jnp.float32)
-            total = total + jnp.where(piece_id == k, part, 0.0)
-        total = total.reshape(sources * CAP, G, 2 * hid)
-        total = jnp.broadcast_to(jnp.sum(total, axis=1, keepdims=True), total.shape)
-        total = total.reshape(sources * B, 2 * hid)
-        gate_proj = total[:, :hid]
-        up_proj = total[:, hid:]
-        hidden = gate_proj / (1.0 + jnp.exp(-gate_proj)) * up_proj
-        piece_h = row_piece(hidden.shape)
-        spread = jnp.concatenate(
-            [jnp.where(piece_h == k, hidden, 0.0).astype(jnp.bfloat16) for k in range(G)], axis=1
-        )
-        down = jnp.concatenate([wd[:, k * piece : (k + 1) * piece] for k in range(G)], axis=0)
-        outb[...] = jnp.dot(spread, down, preferred_element_type=jnp.float32).astype(
-            jnp.bfloat16
-        )
-        for dn, dl in others:
-            give_back(dn, dl).start()
-
-        @pl.when(odd == 1)
-        def _():
-            give_back(0, 0).start()
-
-        @pl.when(odd == 0)
-        def _():
-            own_back.start()
+    def drain(held, sem):
+        pltpu.make_async_copy(held, held, sem).wait()
+
+    @pl.when(sends)
+    def _():
+        drain(recv.at[:near_rows], recv_sem.at[0])
+
+    @pl.when(owns)
+    def _():
+        drain(recv.at[near_rows:], recv_sem.at[1])
+
+    rows = recv[...]
+    piece_id = row_piece((sources * B, 2 * hid))
+    total = jnp.zeros((sources * B, 2 * hid), jnp.float32)
+    for k in range(G):
+        span = slice(k * piece, (k + 1) * piece)
+        both = jnp.concatenate([wg[span, :], wu[span, :]], axis=1)
+        part = jnp.dot(rows, both, preferred_element_type=jnp.float32)
+        total = total + jnp.where(piece_id == k, part, 0.0)
+    total = total.reshape(sources * CAP, G, 2 * hid)
+    total = jnp.broadcast_to(jnp.sum(total, axis=1, keepdims=True), total.shape)
+    total = total.reshape(sources * B, 2 * hid)
+    gate_proj = total[:, :hid]
+    up_proj = total[:, hid:]
+    hidden = gate_proj / (1.0 + jnp.exp(-gate_proj)) * up_proj
+    piece_h = row_piece(hidden.shape)
+    spread = jnp.concatenate(
+        [jnp.where(piece_h == k, hidden, 0.0).astype(jnp.bfloat16) for k in range(G)], axis=1
+    )
+
+    down = jnp.concatenate([wd[:, k * piece : (k + 1) * piece] for k in range(G)], axis=0)
+    outb[...] = jnp.dot(spread, down, preferred_element_type=jnp.float32).astype(jnp.bfloat16)
+
+    @pl.when(sends)
+    def _():
+        pl.semaphore_wait(up_sem, 1)
+        for move in here:
+            for side in range(2):
+                give_back(move, side, 1).start()
+
+    @pl.when(owns)
+    def _():
+        for move in above:
+            for side in range(2):
+                give_back(move, side, 0).start()
 
     @pl.when(owns)
     def _():
@@ -256,9 +281,7 @@
             axis=0,
         )
         mix_ref[...] = jnp.transpose(tall).astype(jnp.bfloat16)
-        for q in range(sources):
-            block = ret.at[q % n_local, pl.ds((q // n_local) * B, B)]
-            pltpu.make_async_copy(block, block, ret_sem.at[q]).wait()
+        drain(ret, ret_sem.at[0])
         summed = ret[0].astype(jnp.float32)
         for m in range(1, n_local):
             summed = summed + ret[m].astype(jnp.float32)
@@ -271,23 +294,13 @@
 
     @pl.when(sends)
     def _():
-        for dn, dl in others:
-            dispatch(dn, dl).wait_send()
-
-        @pl.when(odd == 0)
-        def _():
-            dispatch(0, 0).wait_send()
-
+        drain(recv.at[B:], send_sem.at[0])
+        drain(outb.at[:near_rows], back_sem.at[0])
         comb_copy.wait_send()
 
-    @pl.when(works)
-    def _():
-        for dn, dl in others:
-            give_back(dn, dl).wait_send()
-
-        @pl.when(odd == 1)
-        def _():
-            give_back(0, 0).wait_send()
+    @pl.when(owns)
+    def _():
+        drain(outb.at[near_rows:], back_sem.at[1])
 
 
 def expand_kernel(rows_ref, mix_ref, out_hbm, obuf, sem):
@@ -349,12 +362,13 @@
             pltpu.SemaphoreType.DMA((3,)),
             pltpu.SemaphoreType.DMA((G,)),
             pltpu.SemaphoreType.DMA((3 * SPLIT,)),
-            pltpu.SemaphoreType.DMA((sources,)),
-            pltpu.SemaphoreType.DMA((sources,)),
-            pltpu.SemaphoreType.DMA((sources,)),
-            pltpu.SemaphoreType.DMA((sources,)),
+            pltpu.SemaphoreType.DMA((1,)),
+            pltpu.SemaphoreType.DMA((2,)),
+            pltpu.SemaphoreType.DMA((2,)),
             pltpu.SemaphoreType.DMA((1,)),
             pltpu.SemaphoreType.DMA((1,)),
+            pltpu.SemaphoreType.DMA((1,)),
+            pltpu.SemaphoreType.REGULAR,
         ],
         compiler_params=pltpu.CompilerParams(
             collective_id=0, has_side_effects=True, vmem_limit_bytes=KEEP

time: 15.5 us -> 14.4 us (0.929)
  Pallas kernels: 15.4 us -> 14.3 us
    pallas_call x1, Pallas kernels: 14 us -> 12.9 us  [shards(): pl.pallas_call(functools.partial(relay_kernel, n_section, n_node, n_local...]
where the time goes in v2:
time: 14.4 us; the launch traced here: 14.3 us
  Pallas kernels  14.3 us (99%)
    pallas_call x1, Pallas kernels, shards(): pl.pallas_call(functools.partial(relay_kernel, n_section, n_node, n_local...  12.9 us
    pallas_call x1, Pallas kernels, shards(): pl.pallas_call(expand_kernel, out_shape=jax.ShapeDtypeStruct((tok_dev, wi...  1.34 us

profile of v2, /device:TPU:17, one launch (start us, length us, event | category | flops | bytes accessed | tf_op | source)
XLA Modules:
  0.0 14.3 jit_solution(13853490223233125295)
XLA Ops:
  0.0 12.9 %relay.1 = (bf16[64,896]{1,0:T(8,128)(2,1)S(1)}, bf16[128,128]{1,0:T(8,128)(2,1)S(1)}) custom-call(s32[4]{0:T(128)} %table_hbm.1, s32[8,96]{1,0:T(8,128)} %bitcast.15, f32[8,96]{1,0:T(8,128)} %bitcast.16, bf16[96,7168]{1,0:T(8,128)(2,1)} %bitcast.14, bf16[7168,128]{1,0:T(8,128)(2,1)} %bitcast.11, bf16[7168,128]{1,0:T(8,128)(2,1)} %bitcast.12, ...), custom_call_target="tpu_custom_call" | custom-call | tf_op jit(solution)/shard_map/relay/pallas_call | solution.py:338
  12.9 1.3 %expand.1 = bf16[96,7168]{1,0:T(8,128)(2,1)} custom-call(bf16[64,896]{1,0:T(8,128)(2,1)S(1)} %get-tuple-element.7.rows_ref, bf16[128,128]{1,0:T(8,128)(2,1)S(1)} %get-tuple-element.8.mix_ref), custom_call_target="tpu_custom_call" | custom-call | tf_op jit(solution)/shard_map/expand/pallas_call | solution.py:391

commit v3 on v2

--- a/solution.py
+++ b/solution.py
@@ -44,10 +44,18 @@
         ((dx, dl) for dx in range(chips) for dl in range(n_local)),
         key=lambda d: -min(d[0], chips - d[0]) - min(d[1], n_local - d[1]),
     )
-    here = [d for d in moves if (d[0] + d[1]) % 2 == 0]
-    above = [d for d in moves if (d[0] + d[1]) % 2 == 1]
-    slots = here + above
-    near_rows = len(here) * 2 * B
+    here = [d for d in moves if d[1] % 2 == 1]
+    above = [d for d in moves if d not in here]
+    waves = [[d for d in moves if (d[0] + d[1]) % 2 == odd] for odd in range(2)]
+    waves = [[d for d in wave if d in here] + [d for d in wave if d in above] for wave in waves]
+    slots = waves[0] + waves[1]
+
+    def drain(held, sem):
+        pltpu.make_async_copy(held, held, sem).wait()
+
+    def span(group):
+        low = slots.index(group[0]) * 2 * B
+        return slice(low, low + len(group) * 2 * B)
 
     def place(move, side):
         return (n // 2 + move[0]) % chips * 2 + side, (l + move[1]) % n_local
@@ -90,7 +98,7 @@
             if move != home or flip:
                 greet(s, move, core ^ flip)
 
-    callers = [(back(move), flip) for move in above for flip in range(2)] + [(home, 0)]
+    callers = [(home, flip) for flip in range(2)]
 
     @pl.when(owns)
     def _():
@@ -157,26 +165,21 @@
         c.wait()
     for c in w_copies:
         c.start()
-    def dispatch(move, side, up):
+    def dispatch(move, side):
         j, m = place(move, side)
+        wave = int(move in waves[1])
+        up = int(move in above)
         return pltpu.make_async_remote_copy(
             src_ref=disp.at[pl.ds(pl.multiple_of(j * B, B), B)],
             dst_ref=recv.at[block_of(move, core)],
-            send_sem=send_sem.at[0],
-            recv_sem=recv_sem.at[up],
+            send_sem=send_sem.at[wave],
+            recv_sem=recv_sem.at[wave, up],
             device_id=(s + up, j, m),
             device_id_type=MESH,
         )
 
     def block_of(move, side):
         return pl.ds(pl.multiple_of((slots.index(move) * 2 + side) * B, B), B)
-
-    def own_in():
-        return pltpu.make_async_copy(
-            disp.at[pl.ds(pl.multiple_of(n * B, B), B)],
-            recv.at[block_of(home, core)],
-            recv_sem.at[0],
-        )
 
     comb_copy = pltpu.make_async_remote_copy(
         src_ref=comb_own, dst_ref=comb_in, send_sem=comb_send.at[0], recv_sem=comb_recv.at[0],
@@ -196,23 +199,22 @@
 
     @pl.when(sends)
     def _():
+        for move in waves[0]:
+            for side in range(2):
+                dispatch(move, side).start()
         comb_copy.start()
-        for move in here:
+        pl.semaphore_wait(up_sem, 1)
+        for move in waves[1]:
             for side in range(2):
-                if move != home:
-                    dispatch(move, side, 0).start()
-        for move in above:
-            for side in range(2):
-                dispatch(move, side, 1).start()
-        dispatch(home, 1 - core, 0).start()
-        own_in().start()
-
-    def give_back(move, side, up):
+                dispatch(move, side).start()
+
+    def give_back(move, side):
         qn, ql = place(back(move), side)
+        up = int(move in here)
         return pltpu.make_async_remote_copy(
             src_ref=outb.at[block_of(move, side)],
             dst_ref=ret.at[l, pl.ds(pl.multiple_of(n * B, B), B)],
-            send_sem=back_sem.at[1 - up],
+            send_sem=back_sem.at[up],
             recv_sem=ret_sem.at[0],
             device_id=(s + up, qn, ql),
             device_id_type=MESH,
@@ -221,51 +223,62 @@
     for c in w_copies:
         c.wait()
 
-    def drain(held, sem):
-        pltpu.make_async_copy(held, held, sem).wait()
-
-    @pl.when(sends)
-    def _():
-        drain(recv.at[:near_rows], recv_sem.at[0])
-
-    @pl.when(owns)
-    def _():
-        drain(recv.at[near_rows:], recv_sem.at[1])
-
-    rows = recv[...]
-    piece_id = row_piece((sources * B, 2 * hid))
-    total = jnp.zeros((sources * B, 2 * hid), jnp.float32)
-    for k in range(G):
-        span = slice(k * piece, (k + 1) * piece)
-        both = jnp.concatenate([wg[span, :], wu[span, :]], axis=1)
-        part = jnp.dot(rows, both, preferred_element_type=jnp.float32)
-        total = total + jnp.where(piece_id == k, part, 0.0)
-    total = total.reshape(sources * CAP, G, 2 * hid)
-    total = jnp.broadcast_to(jnp.sum(total, axis=1, keepdims=True), total.shape)
-    total = total.reshape(sources * B, 2 * hid)
-    gate_proj = total[:, :hid]
-    up_proj = total[:, hid:]
-    hidden = gate_proj / (1.0 + jnp.exp(-gate_proj)) * up_proj
-    piece_h = row_piece(hidden.shape)
-    spread = jnp.concatenate(
-        [jnp.where(piece_h == k, hidden, 0.0).astype(jnp.bfloat16) for k in range(G)], axis=1
-    )
-
-    down = jnp.concatenate([wd[:, k * piece : (k + 1) * piece] for k in range(G)], axis=0)
-    outb[...] = jnp.dot(spread, down, preferred_element_type=jnp.float32).astype(jnp.bfloat16)
-
-    @pl.when(sends)
-    def _():
-        pl.semaphore_wait(up_sem, 1)
-        for move in here:
-            for side in range(2):
-                give_back(move, side, 1).start()
-
-    @pl.when(owns)
-    def _():
-        for move in above:
-            for side in range(2):
-                give_back(move, side, 0).start()
+    for number, wave in enumerate(waves):
+        stay = [move for move in wave if move in here]
+        rise = [move for move in wave if move in above]
+
+        @pl.when(sends)
+        def _():
+            drain(recv.at[span(stay)], recv_sem.at[number, 0])
+
+        @pl.when(owns)
+        def _():
+            drain(recv.at[span(rise)], recv_sem.at[number, 1])
+
+        rows = recv[span(wave), :]
+        count = rows.shape[0]
+        piece_id = row_piece((count, 2 * hid))
+        total = jnp.zeros((count, 2 * hid), jnp.float32)
+        for k in range(G):
+            cut = slice(k * piece, (k + 1) * piece)
+            both = jnp.concatenate([wg[cut, :], wu[cut, :]], axis=1)
+            part = jnp.dot(rows, both, preferred_element_type=jnp.float32)
+            total = total + jnp.where(piece_id == k, part, 0.0)
+        total = total.reshape(count // G, G, 2 * hid)
+        total = jnp.broadcast_to(jnp.sum(total, axis=1, keepdims=True), total.shape)
+        total = total.reshape(count, 2 * hid)
+        gate_proj = total[:, :hid]
+        up_proj = total[:, hid:]
+        hidden = gate_proj / (1.0 + jnp.exp(-gate_proj)) * up_proj
+        piece_h = row_piece(hidden.shape)
+        spread = jnp.concatenate(
+            [jnp.where(piece_h == k, hidden, 0.0).astype(jnp.bfloat16) for k in range(G)],
+            axis=1,
+        )
+        down = jnp.concatenate([wd[:, k * piece : (k + 1) * piece] for k in range(G)], axis=0)
+        outb[span(wave), :] = jnp.dot(
+            spread, down, preferred_element_type=jnp.float32
+        ).astype(jnp.bfloat16)
+
+        @pl.when(sends)
+        def _():
+            for move in stay:
+                for side in range(2):
+                    give_back(move, side).start()
+
+        @pl.when(owns)
+        def _():
+            for move in rise:
+                if move != home:
+                    for side in range(2):
+                        give_back(move, side).start()
+                else:
+                    give_back(move, 1 - core).start()
+                    pltpu.make_async_copy(
+                        outb.at[block_of(home, core)],
+                        ret.at[l, pl.ds(pl.multiple_of(n * B, B), B)],
+                        ret_sem.at[0],
+                    ).start()
 
     @pl.when(owns)
     def _():
@@ -294,13 +307,14 @@
 
     @pl.when(sends)
     def _():
-        drain(recv.at[B:], send_sem.at[0])
-        drain(outb.at[:near_rows], back_sem.at[0])
+        drain(recv.at[span(waves[0])], send_sem.at[0])
+        drain(recv.at[span(waves[1])], send_sem.at[1])
+        drain(outb.at[: len(here) * 2 * B], back_sem.at[1])
         comb_copy.wait_send()
 
     @pl.when(owns)
     def _():
-        drain(outb.at[near_rows:], back_sem.at[1])
+        drain(outb.at[: len(above) * 2 * B - B], back_sem.at[0])
 
 
 def expand_kernel(rows_ref, mix_ref, out_hbm, obuf, sem):
@@ -362,8 +376,8 @@
             pltpu.SemaphoreType.DMA((3,)),
             pltpu.SemaphoreType.DMA((G,)),
             pltpu.SemaphoreType.DMA((3 * SPLIT,)),
-            pltpu.SemaphoreType.DMA((1,)),
             pltpu.SemaphoreType.DMA((2,)),
+            pltpu.SemaphoreType.DMA((2, 2)),
             pltpu.SemaphoreType.DMA((2,)),
             pltpu.SemaphoreType.DMA((1,)),
             pltpu.SemaphoreType.DMA((1,)),

time: 14.4 us -> 13.7 us (0.951)
  Pallas kernels: 14.3 us -> 13.5 us
    pallas_call x1, Pallas kernels: 12.9 us -> 12.2 us  [shards(): pl.pallas_call(functools.partial(relay_kernel, n_section, n_node, n_local...]
where the time goes in v3:
time: 13.7 us; the launch traced here: 13.5 us
  Pallas kernels  13.5 us (99%)
    pallas_call x1, Pallas kernels, shards(): pl.pallas_call(functools.partial(relay_kernel, n_section, n_node, n_local...  12.2 us
    pallas_call x1, Pallas kernels, shards(): pl.pallas_call(expand_kernel, out_shape=jax.ShapeDtypeStruct((tok_dev, wi...  1.34 us

profile of v3, /device:TPU:17, one launch (start us, length us, event | category | flops | bytes accessed | tf_op | source)
XLA Modules:
  0.0 13.5 jit_solution(1109997070891162218)
XLA Ops:
  0.0 12.2 %relay.1 = (bf16[64,896]{1,0:T(8,128)(2,1)S(1)}, bf16[128,128]{1,0:T(8,128)(2,1)S(1)}) custom-call(s32[4]{0:T(128)} %table_hbm.1, s32[8,96]{1,0:T(8,128)} %bitcast.15, f32[8,96]{1,0:T(8,128)} %bitcast.16, bf16[96,7168]{1,0:T(8,128)(2,1)} %bitcast.14, bf16[7168,128]{1,0:T(8,128)(2,1)} %bitcast.11, bf16[7168,128]{1,0:T(8,128)(2,1)} %bitcast.12, ...), custom_call_target="tpu_custom_call" | custom-call | tf_op jit(solution)/shard_map/relay/pallas_call | solution.py:352
  12.2 1.3 %expand.1 = bf16[96,7168]{1,0:T(8,128)(2,1)} custom-call(bf16[64,896]{1,0:T(8,128)(2,1)S(1)} %get-tuple-element.7.rows_ref, bf16[128,128]{1,0:T(8,128)(2,1)S(1)} %get-tuple-element.8.mix_ref), custom_call_target="tpu_custom_call" | custom-call | tf_op jit(solution)/shard_map/expand/pallas_call | solution.py:405

commit v4 on v3

--- a/solution.py
+++ b/solution.py
@@ -12,11 +12,16 @@
 B = CAP * G
 KEEP = 24 * 1024 * 1024
 SPLIT = 4
+IN = 512
 MESH = pl.DeviceIdType.MESH
 
 
 def row_piece(shape):
     return lax.broadcasted_iota(jnp.int32, shape, 0) % G
+
+
+def chunks(piece, step):
+    return [(low, min(low + step, piece)) for low in range(0, piece, step)]
 
 
 def relay_kernel(
@@ -165,15 +170,15 @@
         c.wait()
     for c in w_copies:
         c.start()
-    def dispatch(move, side):
+    def dispatch(move, side, low, high):
         j, m = place(move, side)
         wave = int(move in waves[1])
         up = int(move in above)
         return pltpu.make_async_remote_copy(
-            src_ref=disp.at[pl.ds(pl.multiple_of(j * B, B), B)],
-            dst_ref=recv.at[block_of(move, core)],
+            src_ref=disp.at[pl.ds(pl.multiple_of(j * B, B), B), low:high],
+            dst_ref=recv.at[block_of(move, core), low:high],
             send_sem=send_sem.at[wave],
-            recv_sem=recv_sem.at[wave, up],
+            recv_sem=recv_sem.at[wave, up, low // IN],
             device_id=(s + up, j, m),
             device_id_type=MESH,
         )
@@ -185,13 +190,23 @@
         src_ref=comb_own, dst_ref=comb_in, send_sem=comb_send.at[0], recv_sem=comb_recv.at[0],
         device_id=(s + 1, n, l), device_id_type=MESH,
     )
-    disp[...] = jnp.dot(select, tok[...], preferred_element_type=jnp.float32).astype(
-        jnp.bfloat16
-    )
-    pl.semaphore_wait(
-        barrier,
-        sources - 1 + len(callers) * sends.astype(jnp.int32) + owns.astype(jnp.int32),
-    )
+    for low, high in chunks(piece, IN):
+        disp[:, low:high] = jnp.dot(
+            select, tok[:, low:high], preferred_element_type=jnp.float32
+        ).astype(jnp.bfloat16)
+        if low == 0:
+            pl.semaphore_wait(
+                barrier,
+                sources - 1
+                + len(callers) * sends.astype(jnp.int32)
+                + owns.astype(jnp.int32),
+            )
+
+        @pl.when(sends)
+        def _():
+            for move in waves[0]:
+                for side in range(2):
+                    dispatch(move, side, low, high).start()
 
     @pl.when(owns)
     def _():
@@ -199,21 +214,25 @@
 
     @pl.when(sends)
     def _():
-        for move in waves[0]:
-            for side in range(2):
-                dispatch(move, side).start()
         comb_copy.start()
+        for low, high in chunks(piece, IN):
+            for move in waves[1]:
+                if move in here:
+                    for side in range(2):
+                        dispatch(move, side, low, high).start()
         pl.semaphore_wait(up_sem, 1)
-        for move in waves[1]:
-            for side in range(2):
-                dispatch(move, side).start()
-
-    def give_back(move, side):
+        for low, high in chunks(piece, IN):
+            for move in waves[1]:
+                if move in above:
+                    for side in range(2):
+                        dispatch(move, side, low, high).start()
+
+    def give_back(move, side, low, high):
         qn, ql = place(back(move), side)
         up = int(move in here)
         return pltpu.make_async_remote_copy(
-            src_ref=outb.at[block_of(move, side)],
-            dst_ref=ret.at[l, pl.ds(pl.multiple_of(n * B, B), B)],
+            src_ref=outb.at[block_of(move, side), low:high],
+            dst_ref=ret.at[l, pl.ds(pl.multiple_of(n * B, B), B), low:high],
             send_sem=back_sem.at[up],
             recv_sem=ret_sem.at[0],
             device_id=(s + up, qn, ql),
@@ -227,23 +246,25 @@
         stay = [move for move in wave if move in here]
         rise = [move for move in wave if move in above]
 
-        @pl.when(sends)
-        def _():
-            drain(recv.at[span(stay)], recv_sem.at[number, 0])
-
-        @pl.when(owns)
-        def _():
-            drain(recv.at[span(rise)], recv_sem.at[number, 1])
-
-        rows = recv[span(wave), :]
-        count = rows.shape[0]
+        count = len(wave) * 2 * B
         piece_id = row_piece((count, 2 * hid))
         total = jnp.zeros((count, 2 * hid), jnp.float32)
-        for k in range(G):
-            cut = slice(k * piece, (k + 1) * piece)
-            both = jnp.concatenate([wg[cut, :], wu[cut, :]], axis=1)
-            part = jnp.dot(rows, both, preferred_element_type=jnp.float32)
-            total = total + jnp.where(piece_id == k, part, 0.0)
+        for low, high in chunks(piece, IN):
+
+            @pl.when(sends)
+            def _():
+                drain(recv.at[span(stay), low:high], recv_sem.at[number, 0, low // IN])
+
+            @pl.when(owns)
+            def _():
+                drain(recv.at[span(rise), low:high], recv_sem.at[number, 1, low // IN])
+
+            rows = recv[span(wave), low:high]
+            for k in range(G):
+                cut = slice(k * piece + low, k * piece + high)
+                both = jnp.concatenate([wg[cut, :], wu[cut, :]], axis=1)
+                part = jnp.dot(rows, both, preferred_element_type=jnp.float32)
+                total = total + jnp.where(piece_id == k, part, 0.0)
         total = total.reshape(count // G, G, 2 * hid)
         total = jnp.broadcast_to(jnp.sum(total, axis=1, keepdims=True), total.shape)
         total = total.reshape(count, 2 * hid)
@@ -255,30 +276,33 @@
             [jnp.where(piece_h == k, hidden, 0.0).astype(jnp.bfloat16) for k in range(G)],
             axis=1,
         )
-        down = jnp.concatenate([wd[:, k * piece : (k + 1) * piece] for k in range(G)], axis=0)
-        outb[span(wave), :] = jnp.dot(
-            spread, down, preferred_element_type=jnp.float32
-        ).astype(jnp.bfloat16)
-
-        @pl.when(sends)
-        def _():
-            for move in stay:
-                for side in range(2):
-                    give_back(move, side).start()
-
-        @pl.when(owns)
-        def _():
-            for move in rise:
-                if move != home:
+        for low, high in chunks(piece, piece):
+            down = jnp.concatenate(
+                [wd[:, k * piece + low : k * piece + high] for k in range(G)], axis=0
+            )
+            outb[span(wave), low:high] = jnp.dot(
+                spread, down, preferred_element_type=jnp.float32
+            ).astype(jnp.bfloat16)
+
+            @pl.when(sends)
+            def _():
+                for move in stay:
                     for side in range(2):
-                        give_back(move, side).start()
-                else:
-                    give_back(move, 1 - core).start()
-                    pltpu.make_async_copy(
-                        outb.at[block_of(home, core)],
-                        ret.at[l, pl.ds(pl.multiple_of(n * B, B), B)],
-                        ret_sem.at[0],
-                    ).start()
+                        give_back(move, side, low, high).start()
+
+            @pl.when(owns)
+            def _():
+                for move in rise:
+                    if move != home:
+                        for side in range(2):
+                            give_back(move, side, low, high).start()
+                    else:
+                        give_back(move, 1 - core, low, high).start()
+                        pltpu.make_async_copy(
+                            outb.at[block_of(home, core), low:high],
+                            ret.at[l, pl.ds(pl.multiple_of(n * B, B), B), low:high],
+                            ret_sem.at[0],
+                        ).start()
 
     @pl.when(owns)
     def _():
@@ -377,7 +401,7 @@
             pltpu.SemaphoreType.DMA((G,)),
             pltpu.SemaphoreType.DMA((3 * SPLIT,)),
             pltpu.SemaphoreType.DMA((2,)),
-            pltpu.SemaphoreType.DMA((2, 2)),
+            pltpu.SemaphoreType.DMA((2, 2, len(chunks(piece, IN)))),
             pltpu.SemaphoreType.DMA((2,)),
             pltpu.SemaphoreType.DMA((1,)),
             pltpu.SemaphoreType.DMA((1,)),

time: 13.7 us -> 13.7 us (level)
  no operation moved by 1% of the time
where the time goes in v4:
time: 13.7 us; the launch traced here: 13.5 us
  Pallas kernels  13.5 us (99%)
    pallas_call x1, Pallas kernels, shards(): pl.pallas_call(functools.partial(relay_kernel, n_section, n_node, n_local...  12.2 us
    pallas_call x1, Pallas kernels, shards(): pl.pallas_call(expand_kernel, out_shape=jax.ShapeDtypeStruct((tok_dev, wi...  1.34 us

profile of v4, /device:TPU:17, one launch (start us, length us, event | category | flops | bytes accessed | tf_op | source)
XLA Modules:
  0.0 13.5 jit_solution(9847215762855949208)
XLA Ops:
  0.0 12.2 %relay.1 = (bf16[64,896]{1,0:T(8,128)(2,1)S(1)}, bf16[128,128]{1,0:T(8,128)(2,1)S(1)}) custom-call(s32[4]{0:T(128)} %table_hbm.1, s32[8,96]{1,0:T(8,128)} %bitcast.15, f32[8,96]{1,0:T(8,128)} %bitcast.16, bf16[96,7168]{1,0:T(8,128)(2,1)} %bitcast.14, bf16[7168,128]{1,0:T(8,128)(2,1)} %bitcast.11, bf16[7168,128]{1,0:T(8,128)(2,1)} %bitcast.12, ...), custom_call_target="tpu_custom_call" | custom-call | tf_op jit(solution)/shard_map/relay/pallas_call | solution.py:376
  12.2 1.3 %expand.1 = bf16[96,7168]{1,0:T(8,128)(2,1)} custom-call(bf16[64,896]{1,0:T(8,128)(2,1)S(1)} %get-tuple-element.7.rows_ref, bf16[128,128]{1,0:T(8,128)(2,1)S(1)} %get-tuple-element.8.mix_ref), custom_call_target="tpu_custom_call" | custom-call | tf_op jit(solution)/shard_map/expand/pallas_call | solution.py:429

commit v5 on v4

--- a/solution.py
+++ b/solution.py
@@ -12,7 +12,7 @@
 B = CAP * G
 KEEP = 24 * 1024 * 1024
 SPLIT = 4
-IN = 512
+LANES = 512
 MESH = pl.DeviceIdType.MESH
 
 
@@ -178,7 +178,7 @@
             src_ref=disp.at[pl.ds(pl.multiple_of(j * B, B), B), low:high],
             dst_ref=recv.at[block_of(move, core), low:high],
             send_sem=send_sem.at[wave],
-            recv_sem=recv_sem.at[wave, up, low // IN],
+            recv_sem=recv_sem.at[wave, up, low // LANES],
             device_id=(s + up, j, m),
             device_id_type=MESH,
         )
@@ -190,7 +190,7 @@
         src_ref=comb_own, dst_ref=comb_in, send_sem=comb_send.at[0], recv_sem=comb_recv.at[0],
         device_id=(s + 1, n, l), device_id_type=MESH,
     )
-    for low, high in chunks(piece, IN):
+    for low, high in chunks(piece, LANES):
         disp[:, low:high] = jnp.dot(
             select, tok[:, low:high], preferred_element_type=jnp.float32
         ).astype(jnp.bfloat16)
@@ -215,13 +215,13 @@
     @pl.when(sends)
     def _():
         comb_copy.start()
-        for low, high in chunks(piece, IN):
+        for low, high in chunks(piece, LANES):
             for move in waves[1]:
                 if move in here:
                     for side in range(2):
                         dispatch(move, side, low, high).start()
         pl.semaphore_wait(up_sem, 1)
-        for low, high in chunks(piece, IN):
+        for low, high in chunks(piece, LANES):
             for move in waves[1]:
                 if move in above:
                     for side in range(2):
@@ -249,15 +249,15 @@
         count = len(wave) * 2 * B
         piece_id = row_piece((count, 2 * hid))
         total = jnp.zeros((count, 2 * hid), jnp.float32)
-        for low, high in chunks(piece, IN):
+        for low, high in chunks(piece, LANES):
 
             @pl.when(sends)
             def _():
-                drain(recv.at[span(stay), low:high], recv_sem.at[number, 0, low // IN])
+                drain(recv.at[span(stay), low:high], recv_sem.at[number, 0, low // LANES])
 
             @pl.when(owns)
             def _():
-                drain(recv.at[span(rise), low:high], recv_sem.at[number, 1, low // IN])
+                drain(recv.at[span(rise), low:high], recv_sem.at[number, 1, low // LANES])
 
             rows = recv[span(wave), low:high]
             for k in range(G):
@@ -276,7 +276,7 @@
             [jnp.where(piece_h == k, hidden, 0.0).astype(jnp.bfloat16) for k in range(G)],
             axis=1,
         )
-        for low, high in chunks(piece, piece):
+        for low, high in chunks(piece, LANES):
             down = jnp.concatenate(
                 [wd[:, k * piece + low : k * piece + high] for k in range(G)], axis=0
             )
@@ -401,7 +401,7 @@
             pltpu.SemaphoreType.DMA((G,)),
             pltpu.SemaphoreType.DMA((3 * SPLIT,)),
             pltpu.SemaphoreType.DMA((2,)),
-            pltpu.SemaphoreType.DMA((2, 2, len(chunks(piece, IN)))),
+            pltpu.SemaphoreType.DMA((2, 2, len(chunks(piece, LANES)))),
             pltpu.SemaphoreType.DMA((2,)),
             pltpu.SemaphoreType.DMA((1,)),
             pltpu.SemaphoreType.DMA((1,)),

time: 13.7 us -> 13.7 us (level)
  no operation moved by 1% of the time
where the time goes in v5:
time: 13.7 us; the launch traced here: 13.5 us
  Pallas kernels  13.5 us (99%)
    pallas_call x1, Pallas kernels, shards(): pl.pallas_call(functools.partial(relay_kernel, n_section, n_node, n_local...  12.1 us
    pallas_call x1, Pallas kernels, shards(): pl.pallas_call(expand_kernel, out_shape=jax.ShapeDtypeStruct((tok_dev, wi...  1.34 us

profile of v5, /device:TPU:17, one launch (start us, length us, event | category | flops | bytes accessed | tf_op | source)
XLA Modules:
  0.0 13.5 jit_solution(15029115552504552850)
XLA Ops:
  0.0 12.1 %relay.1 = (bf16[64,896]{1,0:T(8,128)(2,1)S(1)}, bf16[128,128]{1,0:T(8,128)(2,1)S(1)}) custom-call(s32[4]{0:T(128)} %table_hbm.1, s32[8,96]{1,0:T(8,128)} %bitcast.15, f32[8,96]{1,0:T(8,128)} %bitcast.16, bf16[96,7168]{1,0:T(8,128)(2,1)} %bitcast.14, bf16[7168,128]{1,0:T(8,128)(2,1)} %bitcast.11, bf16[7168,128]{1,0:T(8,128)(2,1)} %bitcast.12, ...), custom_call_target="tpu_custom_call" | custom-call | tf_op jit(solution)/shard_map/relay/pallas_call | solution.py:376
  12.1 1.3 %expand.1 = bf16[96,7168]{1,0:T(8,128)(2,1)} custom-call(bf16[64,896]{1,0:T(8,128)(2,1)S(1)} %get-tuple-element.7.rows_ref, bf16[128,128]{1,0:T(8,128)(2,1)S(1)} %get-tuple-element.8.mix_ref), custom_call_target="tpu_custom_call" | custom-call | tf_op jit(solution)/shard_map/expand/pallas_call | solution.py:429
